TPU v7x, 32 devices: a whole 2x2x4 slice. The times are simulated.
32 devices in a mesh: groups: 2 (over x), blk: 4 (over y, core), col: 4 (over z).
Axes of the slice: x: 2, y: 2, z: 4, core: 2. Of those that a mesh axis runs over, the one named last changes fastest.
Arguments:
- pair_block: bfloat16 [4096, 16384], P(('groups', 'blk'), 'col'), parts along dimension 0, may hold values from -1.5 to 1.5
- occ_energy: float32 [2], P('groups'), parts along dimension 0, may hold values from -1.5 to -0.3
- virt_energy: float32 [4096], P('groups'), parts along dimension 0, may hold values from 0.2 to 3
- frequency: float32 [2], P('groups'), parts along dimension 0, may hold values from 0.2 to 2
Outputs:
- dielectric: float32 [32768, 16384], P(('groups', 'col'), 'blk'), parts along dimension 0
There are 2 independent parts, one for each index of `groups`. A program takes and returns all parts, laid end to end along the dimension named above; each array names one. Nothing has to cross between parts.
All inputs are finite; a program needn't handle non-finite values.
Results may differ from a plain program's by a relative error of at most 0.0027.
Values may be sent and summed in bfloat16 or wider, within the bound.
A program may use at most 192 MiB of HBM per device.

v0:
```python
import functools

import jax
import jax.numpy as jnp
from jax import lax
from jax.experimental import pallas as pl
from jax.experimental.pallas import tpu as pltpu
from jax.sharding import PartitionSpec as P

MESH = pl.DeviceIdType.MESH
CHUNKS = 8
TO_Y, TO_SIB, FWD_SIB, ECHO, PART0, LOCAL0, ON_XB, LINE0, LINE1, CROSS0, CROSS1 = 0, 1, 2, 3, 4, 8, 12, 16, 17, 18, 19


def pair_weights(occ_energy, virt_energy, frequency):
    gap = (virt_energy[None, :] - occ_energy[:, None]).reshape(-1)
    return 2.0 * gap / (gap * gap + frequency[0] * frequency[0])


def gather_kernel(x_ref, xz, xb, tr, send, rz, rb, rt):
    rows = x_ref.shape[0]
    step_rows = rows // CHUNKS
    g, b, z = lax.axis_index("groups"), lax.axis_index("blk"), lax.axis_index("col")
    last = lax.axis_size("col") - 1
    y, k = b // 2, b % 2
    u, v = k + y - 2 * y * k, z + y * (last - 2 * z)
    tu, tv = 1 - u, last - v
    dz = 1 - 2 * y
    own, sib, opp, dia = b, 2 * y + 1 - k, 2 * (1 - y) + k, 2 * (1 - y) + 1 - k
    first = 2 * y + y
    second = 2 * y + 1 - y
    far0, far1 = 2 * (1 - y) + y, 2 * (1 - y) + 1 - y

    def at(ref, slot, j):
        return ref.at[pl.ds(pl.multiple_of(slot * rows + j * step_rows, step_rows), step_rows)]

    def copy(src, dst, ssem, rsem, dev):
        return pltpu.make_async_remote_copy(
            src_ref=src, dst_ref=dst, send_sem=ssem, recv_sem=rsem, device_id=(g, dev[0], dev[1]), device_id_type=MESH
        )

    def to(kind, j, src, ref, rsem, slot, dev, lane=0):
        return copy(src, at(ref, slot, j), send.at[kind + lane, j], rsem.at[slot, j], dev)

    def arrived(ref, rsem, slot, j):
        copy(at(ref, slot, j), at(ref, slot, j), send.at[0, j], rsem.at[slot, j], (sib, z)).wait_recv()

    source = v == u
    feeds_sib = v == 1 - u
    tz = -dz
    to_sib = (sib, z)
    hop1 = (b, z + dz * (1 - 2 * u))
    up = (b, z + dz)
    down = (b, z - dz)
    line = (b, z + tz)
    cross0, cross1 = (2 * (1 - y) + 1 - y, z), (2 * (1 - y) + y, z)

    def spread(j, src, shard, lane):
        yield source, to(PART0, j, src, xb, rb, shard, hop1, lane)
        yield feeds_sib, to(LOCAL0, j, src, xb, rb, shard, to_sib, lane)
        if lane < 2:
            yield (u == 1) & (v == 1), to(ON_XB, j, src, xb, rb, shard, up, lane)

    def own_sends(j):
        src = x_ref.at[pl.ds(pl.multiple_of(j * step_rows, step_rows), step_rows)]
        yield True, to(TO_SIB, j, src, xz, rz, own, to_sib)
        yield True, to(TO_Y, j, src, xz, rz, own, (opp, z))
        yield tv == 0, to(LINE0, j, src, tr, rt, 0, line)
        yield tv == 1, to(LINE1, j, src, tr, rt, 1, line)
        yield from spread(j, src, own, 0)

    def sib_sends(j):
        src = at(xz, sib, j)
        yield True, to(ECHO, j, src, xz, rz, sib, to_sib)
        yield from spread(j, src, sib, 1)

    def opp_sends(j):
        src = at(xz, opp, j)
        yield True, to(FWD_SIB, j, src, xz, rz, opp, to_sib)
        yield from spread(j, src, opp, 2)

    def dia_sends(j):
        yield from spread(j, at(xz, dia, j), dia, 3)

    passes = [
        (1, (tv == 1), tr, rt, 0, lambda j: to(LINE0, j, at(tr, 0, j), tr, rt, 0, line)),
        (1, (u == 0) & (v == 1), xb, rb, first, lambda j: to(ON_XB, j, at(xb, first, j), xb, rb, first, up, 0)),
        (2, (u == 1) & (v == 2), xb, rb, second, lambda j: to(ON_XB, j, at(xb, second, j), xb, rb, second, up, 0)),
        (2, (tv == 2), tr, rt, 1, lambda j: to(CROSS1, j, at(tr, 1, j), xb, rb, own, cross1)),
        (3, (u == 0) & (v == 2), xb, rb, first, lambda j: to(ON_XB, j, at(xb, first, j), xb, rb, first, up, 0)),
        (9, (u == 0) & (v == 1), xb, rb, second, lambda j: to(ON_XB, j, at(xb, second, j), xb, rb, second, up, 1)),
        (10, (u == 1) & (v == 2), xb, rb, first, lambda j: to(ON_XB, j, at(xb, first, j), xb, rb, first, up, 1)),
        (10, (tv == 2), tr, rt, 0, lambda j: to(LINE0, j, at(tr, 0, j), tr, rt, 0, line)),
        (11, (tv == 3), tr, rt, 0, lambda j: to(CROSS0, j, at(tr, 0, j), xb, rb, own, cross0)),
        (11, (u == 0) & (v == 2), xb, rb, second, lambda j: to(ON_XB, j, at(xb, second, j), xb, rb, second, up, 1)),
        (11, (u == 1) & (v == 2), xb, rb, far0, lambda j: to(ON_XB, j, at(xb, far0, j), xb, rb, far0, up, 2)),
        (11, (u == 1) & (v == 2), xb, rb, far1, lambda j: to(ON_XB, j, at(xb, far1, j), xb, rb, far1, up, 3)),
        (13, (u == 0) & (v == 3), xb, rb, far0, lambda j: to(ON_XB, j, at(xb, far0, j), xb, rb, far0, down, 2)),
        (13, (u == 0) & (v == 3), xb, rb, far1, lambda j: to(ON_XB, j, at(xb, far1, j), xb, rb, far1, down, 3)),
    ]

    def when(cond, f):
        if cond is True:
            f()
        else:
            pl.when(cond)(f)

    def start_all(sends):
        for cond, c in sends:
            when(cond, c.start)

    barrier = pltpu.get_barrier_semaphore()
    peers = [(sib, z), (opp, z), (dia, z)] + [(b, lax.rem(z + i, last + 1)) for i in range(1, last + 1)]
    for dev in peers:
        pl.semaphore_signal(barrier, inc=1, device_id=(g,) + dev, device_id_type=MESH)
    pl.semaphore_wait(barrier, len(peers))

    @pl.loop(0, CHUNKS)
    def _(j):
        start_all(own_sends(j))

    @pl.loop(0, CHUNKS)
    def _(j):
        arrived(xz, rz, sib, j)
        start_all(sib_sends(j))

    @pl.loop(0, CHUNKS + 13)
    def _(t):
        @pl.when(t < CHUNKS)
        def _():
            arrived(xz, rz, opp, t)
            start_all(opp_sends(t))

        @pl.when((t >= 1) & (t < CHUNKS + 1))
        def _():
            arrived(xz, rz, dia, t - 1)
            start_all(dia_sends(t - 1))

        for lag, role, ref, rsem, slot, send_on in passes:

            @pl.when(role & (t >= lag) & (t < lag + CHUNKS))
            def _():
                arrived(ref, rsem, slot, t - lag)
                send_on(t - lag).start()

    @pl.loop(0, CHUNKS)
    def _(j):
        arrived(xz, rz, own, j)
        near = ((u == 0) & (v == 1)) | (v == 2)
        far = ((u == 1) & (v == 2)) | ((u == 0) & (v == 3))

        @pl.when(jnp.logical_not(near))
        def _():
            arrived(xb, rb, first, j)
            arrived(xb, rb, second, j)

        @pl.when(jnp.logical_not(far))
        def _():
            arrived(xb, rb, far0, j)
            arrived(xb, rb, far1, j)

        for sends in (own_sends(j), sib_sends(j), opp_sends(j), dia_sends(j)):
            for cond, c in sends:
                when(cond, c.wait_send)
        for _, role, _, _, _, send_on in passes:
            pl.when(role)(send_on(j).wait_send)


def gather_both(pair_block):
    rows, cols = pair_block.shape
    full = jax.ShapeDtypeStruct((4 * rows, cols), pair_block.dtype)
    return pl.pallas_call(
        gather_kernel,
        out_shape=(full, full, jax.ShapeDtypeStruct((2 * rows, cols), pair_block.dtype)),
        in_specs=[pl.BlockSpec(memory_space=pl.ANY)],
        out_specs=[pl.BlockSpec(memory_space=pl.ANY)] * 3,
        scratch_shapes=[
            pltpu.SemaphoreType.DMA((20, CHUNKS)),
            pltpu.SemaphoreType.DMA((4, CHUNKS)),
            pltpu.SemaphoreType.DMA((4, CHUNKS)),
            pltpu.SemaphoreType.DMA((2, CHUNKS)),
        ],
        compiler_params=pltpu.CompilerParams(collective_id=0, has_side_effects=True),
    )(pair_block)


def shards(square, pair_block, occ_energy, virt_energy, frequency):
    weights = pair_weights(occ_energy, virt_energy, frequency)
    if square:
        own_columns, column_slab, _ = gather_both(pair_block)
    else:
        row_full = lax.all_gather(pair_block, "col", axis=1, tiled=True)
        column_slab = lax.all_to_all(row_full, "blk", split_axis=1, concat_axis=0, tiled=True)
        own_columns = lax.all_gather(pair_block, "blk", axis=0, tiled=True)
    scaled = (own_columns.astype(jnp.float32) * weights[:, None]).astype(jnp.bfloat16)
    return lax.dot_general(
        scaled, column_slab, (((0,), (0,)), ((), ())), preferred_element_type=jnp.float32
    )


def solution(mesh):
    square = mesh.shape["blk"] == 4 and mesh.shape["col"] == 4
    return jax.shard_map(
        functools.partial(shards, square),
        mesh=mesh,
        in_specs=(P(("groups", "blk"), "col"), P("groups"), P("groups"), P("groups")),
        out_specs=P(("groups", "col"), "blk"),
        check_vma=False,
    )
```

profile of v0, /device:TPU:16, one launch (start us, length us, event | category | flops | bytes accessed | tf_op | source)
XLA Modules:
  0.0 421.9 jit_solution(9831215618635554082)
XLA Ops:
  1.3 0.7 add_divide_fusion
  2.0 338.7 %shard_map.46 = (bf16[2048,4096]{1,0:T(8,128)(2,1)}, bf16[2048,4096]{1,0:T(8,128)(2,1)}, bf16[1024,4096]{1,0:T(8,128)(2,1)}) custom-call(bf16[512,4096]{1,0:T(8,128)(2,1)} %x_ref.1), custom_call_target="tpu_custom_call" | custom-call | tf_op jit(solution)/shard_map/pallas_call | solution.py:172
  340.7 81.1 %fusion = f32[4096,4096]{1,0:T(8,128)} fusion(bf16[2048,4096]{1,0:T(8,128)(2,1)} %get-tuple-element.8, bf16[2048,4096]{1,0:T(8,128)(2,1)} %get-tuple-element.7, f32[2048]{0:T(1024)S(1)} %add_divide_fusion), kind=kOutput, calls=%fused_computation.1 | convolution fusion | flops 68744642560 | bytes 100671488 | tf_op jit(solution)/shard_map/dot_general | solution.py:196
where the time goes:
time: 422 us
  Pallas kernels  339 us (80%)
  matrix products  81.1 us (19%)
    pallas_call x1, Pallas kernels, gather_both(): pl.pallas_call(gather_kernel, out_shape=(full, full, jax.ShapeDtypeStruct...  339 us
    dot_general x1, matrix products, shards(): lax.dot_general(scaled, column_slab, (((0,), (0,)), ((), ())), preferred_...  81.1 us

commit v1 on v0

v1 whole, which is shorter than its diff:
```python
import functools

import jax
import jax.numpy as jnp
from jax import lax
from jax.experimental import pallas as pl
from jax.experimental.pallas import tpu as pltpu
from jax.sharding import PartitionSpec as P

MESH = pl.DeviceIdType.MESH
CHUNKS = 16
UNITS = 8
TILES = 8
EARLY = 5
FIRST = 21
TICKS = 3 * CHUNKS + 4
TO_SIB, TO_OPP, UP, DOWN, FWD, DOWN_OPP, UP_OPP, UP_DIA, HOP_OWN, HOP_SIB, HOP_OPP, HOP_DIA, PASS, CROSS = range(14)
BOUNCE = 4


def pair_weights(occ_energy, virt_energy, frequency):
    gap = (virt_energy[None, :] - occ_energy[:, None]).reshape(-1)
    return 2.0 * gap / (gap * gap + frequency[0] * frequency[0])


def place():
    b, z = lax.axis_index("blk"), lax.axis_index("col")
    last = lax.axis_size("col") - 1
    y, k = b // 2, b % 2
    u, v = k + y - 2 * y * k, z + y * (last - 2 * z)
    return b, z, y, k, u, v


def when(cond, f):
    if cond is True:
        f()
    else:
        pl.when(cond)(f)


def load_columns(x, xz, xb, dst, sem, at_home, own, n, width):
    rows = x.shape[0]
    cols = pl.ds(pl.multiple_of(n * width, width), width)

    def piece(src, r):
        return pltpu.make_async_copy(src, dst.at[pl.ds(pl.multiple_of(r * rows, rows), rows)], sem.at[r])

    for r in range(4):
        band = pl.ds(r * rows, rows)

        @pl.when(jnp.logical_not(at_home))
        def _():
            piece(xb.at[band, cols], r).start()

        @pl.when(at_home & (own != r))
        def _():
            piece(xz.at[band, cols], r).start()

        @pl.when(at_home & (own == r))
        def _():
            piece(x.at[:, cols], r).start()


def await_columns(xb, dst, sem, rows, width):
    for r in range(4):
        band = pl.ds(r * rows, rows)
        pltpu.make_async_copy(xb.at[band, pl.ds(0, width)], dst.at[band], sem.at[r]).wait()


def gather_kernel(
    x, wt, xz, xb, tr, lhs_out, part,
    lhs, stage, rhs, acc, send, rz, rb, rt, stage_sem, rhs_sem, acc_sem, lhs_sem,
):
    rows, cols = x.shape
    step = cols // CHUNKS
    width = cols // UNITS
    tile = cols // TILES
    g = lax.axis_index("groups")
    b, z, y, k, u, v = place()
    dz = 1 - 2 * y
    own, sib, opp, dia = b, 2 * y + 1 - k, 2 * (1 - y) + k, 2 * (1 - y) + 1 - k
    lead0, lead1 = 3 * y, y + 1
    at_home = u == v

    def at(ref, r, c):
        return ref.at[
            pl.ds(pl.multiple_of(r * rows, rows), rows), pl.ds(pl.multiple_of(c * step, step), step)
        ]

    def copy(src, dst, ssem, rsem, dev):
        return pltpu.make_async_remote_copy(
            src_ref=src, dst_ref=dst, send_sem=ssem, recv_sem=rsem, device_id=(g, dev[0], dev[1]), device_id_type=MESH
        )

    to_sib, to_opp = (sib, z), (opp, z)
    up0, up1 = (lead0, z + dz), (lead1, z + dz)
    down1, down_same = (lead1, z - dz), (b, z - dz)
    across = (3 * (1 - y), z)

    def go(kind, c, src, ref, rsem, r, dev):
        copy(src, at(ref, r, c), send.at[kind, c], rsem.at[r, c], dev).start()

    def arrived(ref, rsem, r, c):
        copy(at(ref, r, c), at(ref, r, c), send.at[0, c], rsem.at[r, c], to_sib).wait_recv()

    hop0 = (u == 0) & ((v == 1) | (v == 2))
    hop1 = (u == 1) & (v == 2)
    lift = (v == 1) & (u == 1)

    barrier = pltpu.get_barrier_semaphore()
    for i in range(16):
        bb, zz = i // 4, i % 4

        @pl.when((bb != b) | (zz != z))
        def _():
            pl.semaphore_signal(barrier, inc=1, device_id=(g, bb, zz), device_id_type=MESH)

    pl.semaphore_wait(barrier, 15)

    def line_own(c):
        src = at(x, 0, c)
        pl.when(v == 1)(lambda: go(UP, c, src, xb, rb, own, up1))
        pl.when(v == 1)(lambda: go(DOWN, c, src, xb, rb, own, down1))

    line_own(0)
    line_own(1)

    @pl.loop(0, CHUNKS)
    def _(c):
        src = at(x, 0, c)
        go(TO_OPP, c, src, xz, rz, own, to_opp)
        pl.when(v == 0)(lambda: go(UP, c, src, xb, rb, own, up0))
        pl.when(v == 3)(lambda: go(DOWN, c, src, tr, rt, 0, down_same))
        go(TO_SIB, c, src, xz, rz, own, to_sib)

    def hop(kind, r, c, dev):
        arrived(xb, rb, r, c)
        go(kind, c, at(xb, r, c), xb, rb, r, dev)

    def end_waits(n):
        for i in range(CHUNKS // UNITS):
            c = n * (CHUNKS // UNITS) + i
            for r in (own, sib):
                pl.when(jnp.logical_not(at_home | hop0 | hop1))(lambda: arrived(xb, rb, r, c))
            for r in (opp, dia):
                pl.when(jnp.logical_not(at_home | hop1))(lambda: arrived(xb, rb, r, c))

    def stage_load(src):
        return pltpu.make_async_copy(src, stage, stage_sem.at[0])

    def band(ref, r):
        return ref.at[pl.ds(pl.multiple_of(r * rows, rows), rows)]

    def save(n, p, s):
        dst = part.at[pl.ds(pl.multiple_of(n * cols + p * tile, tile), tile)]
        return pltpu.make_async_copy(acc.at[s], dst, acc_sem.at[s])

    lhs_save = pltpu.make_async_copy(lhs, lhs_out, lhs_sem.at[0])

    @pl.loop(0, TICKS)
    def _(t):
        m, phase = t // 3, lax.rem(t, 3)

        @pl.when((t + 2 < CHUNKS) & (t >= 0))
        def _():
            line_own(t + 2)

        @pl.when(t < CHUNKS)
        def _():
            arrived(xz, rz, opp, t)
            src = at(xz, opp, t)
            pl.when(lift)(lambda: go(UP_OPP, t, src, xb, rb, opp, up1))
            pl.when(v == 1)(lambda: go(DOWN_OPP, t, src, xb, rb, opp, down1))
            go(FWD, t, src, xz, rz, opp, to_sib)

            @pl.when((u == 0) & (v == 1))
            def _():
                hop(HOP_OWN, own, t, up0)
                hop(HOP_SIB, sib, t, up0)

        @pl.when((t >= 1) & (t < CHUNKS + 1))
        def _():
            arrived(xz, rz, dia, t - 1)
            pl.when(lift)(lambda: go(UP_DIA, t - 1, at(xz, dia, t - 1), xb, rb, dia, up1))

        late = jnp.where(v == 0, m - 2, t - 2 + v)

        @pl.when((v <= 2) & ((v > 0) | (phase == 0)) & (late >= 0) & (late < CHUNKS))
        def _():
            arrived(tr, rt, 0, late)
            src = at(tr, 0, late)
            pl.when(v >= 1)(lambda: go(PASS, late, src, tr, rt, 0, down_same))
            go(CROSS, late, src, xb, rb, own, across)

        @pl.when(v == 2)
        def _():
            @pl.when(u == 1)
            def _():
                @pl.when(t == 0)
                def _():
                    hop(HOP_OWN, own, 0, up1)
                    hop(HOP_SIB, sib, 0, up1)

                @pl.when(((phase == 0) & (m >= 1) & (m + 1 < CHUNKS)))
                def _():
                    hop(HOP_OWN, own, m + 1, up1)

                @pl.when(t == 1)
                def _():
                    hop(HOP_OWN, own, 1, up1)

                @pl.when((phase == 1) & (m + 1 < CHUNKS))
                def _():
                    hop(HOP_SIB, sib, m + 1, up1)

                @pl.when((phase == 1) & (m < CHUNKS))
                def _():
                    hop(HOP_OPP, opp, m, up1)

                @pl.when((phase == 2) & (m >= 1) & (m <= CHUNKS))
                def _():
                    hop(HOP_DIA, dia, m - 1, up1)

            @pl.when(u == 0)
            def _():
                @pl.when((phase == 0) & (m >= 1) & (m <= CHUNKS))
                def _():
                    hop(HOP_SIB, sib, m - 1, up0)

                @pl.when((phase == 2) & (m < CHUNKS))
                def _():
                    hop(HOP_OWN, own, m, up0)

        @pl.when(t == 5)
        def _():
            @pl.loop(0, CHUNKS)
            def _(c):
                arrived(xz, rz, sib, c)

        fill = (t == 2) | (t == 6) | (t == CHUNKS + 1) | (t == CHUNKS + 2)

        @pl.when(fill)
        def _():
            r = jnp.where(t == 2, own, jnp.where(t == 6, sib, jnp.where(t == CHUNKS + 1, opp, dia)))
            stage_load(x).wait()
            scale = wt[:, pl.ds(pl.multiple_of(r * rows, rows), rows)]

            @pl.loop(0, TILES)
            def _(i):
                p = pl.ds(pl.multiple_of(i * tile, tile), tile)
                turned = stage[:, p].T.astype(jnp.float32) * scale
                lhs[p, pl.ds(pl.multiple_of(r * rows, rows), rows)] = turned.astype(jnp.bfloat16)

        pl.when(t == 1)(lambda: stage_load(x).start())
        pl.when(t == 5)(lambda: stage_load(band(xz, sib)).start())
        pl.when(t == CHUNKS)(lambda: stage_load(band(xz, opp)).start())
        pl.when(t == CHUNKS + 1)(lambda: stage_load(band(xz, dia)).start())
        pl.when(t == CHUNKS + 2)(lambda: lhs_save.start())

        work = t - FIRST
        n, q = work // 4, lax.rem(work, 4)

        @pl.when((work >= 0) & (work < 4 * EARLY))
        def _():
            s = lax.rem(n, 2)

            @pl.when(q == 0)
            def _():
                await_columns(xb, rhs.at[s], rhs_sem.at[s], rows, width)

            for j in range(2):
                p = 2 * q + j
                pl.when(work >= 1)(lambda: save(0, 0, j).wait())
                acc[j] = jnp.dot(
                    lhs[pl.ds(pl.multiple_of(p * tile, tile), tile), :], rhs[s], preferred_element_type=jnp.float32
                )
                save(n, p, j).start()

        ahead = work + 1
        n_ahead = ahead // 4

        @pl.when((ahead >= 0) & (ahead < 4 * EARLY) & (lax.rem(ahead, 4) == 0))
        def _():
            end_waits(n_ahead)
            s = lax.rem(n_ahead, 2)
            load_columns(x, xz, xb, rhs.at[s], rhs_sem.at[s], at_home, own, n_ahead, width)

    for j in range(2):
        save(0, 0, j).wait()
    lhs_save.wait()

    @pl.loop(EARLY, UNITS)
    def _(n):
        end_waits(n)

    sends = [
        (TO_SIB, True), (TO_OPP, True), (FWD, True),
        (UP, v <= 1), (DOWN, (v == 1) | (v == 3)), (DOWN_OPP, v == 1),
        (UP_OPP, lift), (UP_DIA, lift),
        (HOP_OWN, hop0 | hop1), (HOP_SIB, hop0 | hop1), (HOP_OPP, hop1), (HOP_DIA, hop1),
        (PASS, (v == 1) | (v == 2)), (CROSS, v <= 2),
    ]

    @pl.loop(0, CHUNKS)
    def _(c):
        for kind, cond in sends:
            when(cond, lambda: copy(at(x, 0, c), at(xz, 0, c), send.at[kind, c], rz.at[0, c], to_sib).wait_send())


def gather(pair_block, weights):
    rows, cols = pair_block.shape
    width, tile = cols // UNITS, cols // TILES
    bf16, f32 = jnp.bfloat16, jnp.float32
    full = jax.ShapeDtypeStruct((4 * rows, cols), bf16)
    return pl.pallas_call(
        gather_kernel,
        out_shape=(
            full,
            full,
            jax.ShapeDtypeStruct((rows, cols), bf16),
            jax.ShapeDtypeStruct((cols, 4 * rows), bf16),
            jax.ShapeDtypeStruct((EARLY * cols, width), f32),
        ),
        in_specs=[pl.BlockSpec(memory_space=pl.ANY), pl.BlockSpec(memory_space=pltpu.VMEM)],
        out_specs=[pl.BlockSpec(memory_space=pl.ANY)] * 5,
        scratch_shapes=[
            pltpu.VMEM((cols, 4 * rows), bf16),
            pltpu.VMEM((rows, cols), bf16),
            pltpu.VMEM((2, 4 * rows, width), bf16),
            pltpu.VMEM((2, tile, width), f32),
            pltpu.SemaphoreType.DMA((14, CHUNKS)),
            pltpu.SemaphoreType.DMA((4, CHUNKS)),
            pltpu.SemaphoreType.DMA((4, CHUNKS)),
            pltpu.SemaphoreType.DMA((1, CHUNKS)),
            pltpu.SemaphoreType.DMA((1,)),
            pltpu.SemaphoreType.DMA((2, 4)),
            pltpu.SemaphoreType.DMA((2,)),
            pltpu.SemaphoreType.DMA((1,)),
        ],
        compiler_params=pltpu.CompilerParams(collective_id=0, has_side_effects=True),
    )(pair_block, weights[None, :])


def finish_kernel(
    x, xz, xb, lhs_in, part, out,
    lhs, rhs, acc, hold, lhs_sem, rhs_sem, acc_sem, in_sem, out_sem,
):
    rows, cols = x.shape
    width, tile = cols // UNITS, cols // TILES
    late = UNITS - EARLY
    moves = EARLY * TILES // 2
    b, z, y, k, u, v = place()

    def span(i, size):
        return pl.ds(pl.multiple_of(i * size, size), size)

    def take(i):
        s = lax.rem(i, BOUNCE)
        return pltpu.make_async_copy(part.at[span(i, 2 * tile)], hold.at[s], in_sem.at[s])

    def put(i):
        s = lax.rem(i, BOUNCE)
        n, p = i // (TILES // 2), lax.rem(i, TILES // 2)
        return pltpu.make_async_copy(hold.at[s], out.at[span(p, 2 * tile), span(n, width)], out_sem.at[s])

    def fetch(p):
        s = lax.rem(p, 2)
        return pltpu.make_async_copy(lhs_in.at[span(p, tile)], lhs.at[s], lhs_sem.at[s])

    def store(p, n):
        return pltpu.make_async_copy(acc.at[n], out.at[span(p, tile), span(EARLY + n, width)], acc_sem.at[n])

    fetch(0).start()
    for n in range(late):
        load_columns(x, xz, xb, rhs.at[n], rhs_sem.at[n], u == v, b, EARLY + n, width)
    for i in range(2):
        take(i).start()
    fetch(1).start()

    def shift(i):
        @pl.when(i < moves)
        def _():
            take(i).wait()
            put(i).start()

        @pl.when(i + 2 < moves)
        def _():
            pl.when(i + 2 >= BOUNCE)(lambda: put(i + 2 - BOUNCE).wait())
            take(i + 2).start()

    @pl.loop(0, TILES)
    def _(p):
        fetch(p).wait()
        for n in range(late):
            pl.when(p == 0)(lambda: await_columns(xb, rhs.at[n], rhs_sem.at[n], rows, width))
            pl.when(p >= 1)(lambda: store(p - 1, n).wait())
            acc[n] = jnp.dot(lhs[lax.rem(p, 2)], rhs[n], preferred_element_type=jnp.float32)
            store(p, n).start()
            shift(p * late + n)

        pl.when(p + 2 < TILES)(lambda: fetch(p + 2).start())

    for i in range(TILES * late, moves):
        shift(i)
    for n in range(late):
        store(TILES - 1, n).wait()
    for i in range(max(0, moves - BOUNCE), moves):
        put(i).wait()


def finish(pair_block, xz, xb, lhs, part):
    rows, cols = pair_block.shape
    width, tile = cols // UNITS, cols // TILES
    late = UNITS - EARLY
    bf16, f32 = jnp.bfloat16, jnp.float32
    return pl.pallas_call(
        finish_kernel,
        out_shape=jax.ShapeDtypeStruct((cols, cols), f32),
        in_specs=[pl.BlockSpec(memory_space=pl.ANY)] * 5,
        out_specs=pl.BlockSpec(memory_space=pl.ANY),
        scratch_shapes=[
            pltpu.VMEM((2, tile, 4 * rows), bf16),
            pltpu.VMEM((late, 4 * rows, width), bf16),
            pltpu.VMEM((late, tile, width), f32),
            pltpu.VMEM((BOUNCE, 2 * tile, width), f32),
            pltpu.SemaphoreType.DMA((2,)),
            pltpu.SemaphoreType.DMA((late, 4)),
            pltpu.SemaphoreType.DMA((late,)),
            pltpu.SemaphoreType.DMA((BOUNCE,)),
            pltpu.SemaphoreType.DMA((BOUNCE,)),
        ],
    )(pair_block, xz, xb, lhs, part)


def shards(square, pair_block, occ_energy, virt_energy, frequency):
    weights = pair_weights(occ_energy, virt_energy, frequency)
    if square:
        xz, xb, _, lhs, part = gather(pair_block, weights)
        return finish(pair_block, xz, xb, lhs, part)
    row_full = lax.all_gather(pair_block, "col", axis=1, tiled=True)
    column_slab = lax.all_to_all(row_full, "blk", split_axis=1, concat_axis=0, tiled=True)
    own_columns = lax.all_gather(pair_block, "blk", axis=0, tiled=True)
    scaled = (own_columns.astype(jnp.float32) * weights[:, None]).astype(jnp.bfloat16)
    return lax.dot_general(
        scaled, column_slab, (((0,), (0,)), ((), ())), preferred_element_type=jnp.float32
    )


def solution(mesh):
    square = mesh.shape["blk"] == 4 and mesh.shape["col"] == 4
    return jax.shard_map(
        functools.partial(shards, square),
        mesh=mesh,
        in_specs=(P(("groups", "blk"), "col"), P("groups"), P("groups"), P("groups")),
        out_specs=P(("groups", "col"), "blk"),
        check_vma=False,
    )
```

time: 422 us -> 344 us (0.82); the launches traced: 422 us -> 338 us
  matrix products: 81.1 us -> 0 us
    dot_general x1 -> x0, matrix products: 81.1 us -> none  [shards(): lax.dot_general(scaled, column_slab, (((0,), (0,)), ((), ())), preferred_...]
    pallas_call x1 -> x2, Pallas kernels: 339 us -> 336 us  [the longest x1 287 us: gather(): pl.pallas_call(gather_kernel, out_shape=(full, full, jax.ShapeDtypeStruct...]
where the time goes in v1:
time: 344 us; the launch traced here: 338 us
  Pallas kernels  336 us (98%)
    pallas_call x1, Pallas kernels, gather(): pl.pallas_call(gather_kernel, out_shape=(full, full, jax.ShapeDtypeStruct...  287 us
    pallas_call x1, Pallas kernels, finish(): pl.pallas_call(finish_kernel, out_shape=jax.ShapeDtypeStruct((cols, cols)...  49 us

profile of v1, /device:TPU:16, one launch (start us, length us, event | category | flops | bytes accessed | tf_op | source)
XLA Modules:
  0.0 338.2 jit_solution(15100915921571142371)
XLA Ops:
  1.3 1.3 add_divide_fusion
  2.6 286.6 %shard_map.46 = (bf16[2048,4096]{1,0:T(8,128)(2,1)}, bf16[2048,4096]{1,0:T(8,128)(2,1)}, bf16[512,4096]{1,0:T(8,128)(2,1)}, bf16[4096,2048]{1,0:T(8,128)(2,1)}, f32[20480,512]{1,0:T(8,128)}) custom-call(bf16[512,4096]{1,0:T(8,128)(2,1)} %x.3, f32[1,2048]{1,0:T(1,128)} %bitcast.4), custom_call_target="tpu_custom_call" | custom-call | tf_op jit(solution)/shard_map/pallas_call | solution.py:315
  289.2 49.0 %shard_map.47 = f32[4096,4096]{1,0:T(8,128)} custom-call(bf16[512,4096]{1,0:T(8,128)(2,1)} %x.3, bf16[2048,4096]{1,0:T(8,128)(2,1)} %get-tuple-element.9.xz, bf16[2048,4096]{1,0:T(8,128)(2,1)} %get-tuple-element.10.xb, bf16[4096,2048]{1,0:T(8,128)(2,1)} %get-tuple-element.11.lhs_in, f32[20480,512]{1,0:T(8,128)} %get-tuple-element.12.part), custom_call_target="tpu_custom_call" | custom-call | tf_op jit(solution)/shard_map/pallas_call | solution.py:416

commit v2 on v1

v2 whole, which is shorter than its diff:
```python
import functools

import jax
import jax.numpy as jnp
from jax import lax
from jax.experimental import pallas as pl
from jax.experimental.pallas import tpu as pltpu
from jax.sharding import PartitionSpec as P

MESH = pl.DeviceIdType.MESH
CHUNKS = 32
UNITS = 8
TILES = 8
EARLY = 7
FIRST = CHUNKS + 11
HELD = 3 * CHUNKS // 4
TICKS = 3 * CHUNKS + 4
PER_TICK = 32 // CHUNKS
SPAN = TILES // PER_TICK
MIB = 1 << 20
TO_SIB, TO_OPP, UP, DOWN, FWD, DOWN_OPP, UP_OPP, UP_DIA, HOP_OWN, HOP_SIB, HOP_OPP, HOP_DIA, PASS, CROSS = range(14)
SLOTS = 6
STRIPS = 4


def pair_weights(occ_energy, virt_energy, frequency):
    gap = (virt_energy[None, :] - occ_energy[:, None]).reshape(-1)
    return 2.0 * gap / (gap * gap + frequency[0] * frequency[0])


def place():
    b, z = lax.axis_index("blk"), lax.axis_index("col")
    last = lax.axis_size("col") - 1
    y, k = b // 2, b % 2
    u, v = k + y - 2 * y * k, z + y * (last - 2 * z)
    return b, z, y, k, u, v


def when(cond, f):
    if cond is True:
        f()
    else:
        pl.when(cond)(f)


def load_columns(x, xz, xb, dst, sem, at_home, own, n, width):
    rows = x.shape[0]
    cols = pl.ds(pl.multiple_of(n * width, width), width)

    def piece(src, r):
        return pltpu.make_async_copy(src, dst.at[pl.ds(pl.multiple_of(r * rows, rows), rows)], sem.at[r])

    for r in range(4):
        band = pl.ds(r * rows, rows)

        @pl.when(jnp.logical_not(at_home))
        def _():
            piece(xb.at[band, cols], r).start()

        @pl.when(at_home & (own != r))
        def _():
            piece(xz.at[band, cols], r).start()

        @pl.when(at_home & (own == r))
        def _():
            piece(x.at[:, cols], r).start()


def await_columns(xb, dst, sem, rows, width):
    for r in range(4):
        band = pl.ds(r * rows, rows)
        pltpu.make_async_copy(xb.at[band, pl.ds(0, width)], dst.at[band], sem.at[r]).wait()


def gather_kernel(
    x, wt, xz, xb, tr, lhs, kept,
    stage, rhs, send, rz, rb, rt, stage_sem, rhs_sem,
):
    rows, cols = x.shape
    step = cols // CHUNKS
    width = cols // UNITS
    tile = cols // TILES
    g = lax.axis_index("groups")
    b, z, y, k, u, v = place()
    dz = 1 - 2 * y
    own, sib, opp, dia = b, 2 * y + 1 - k, 2 * (1 - y) + k, 2 * (1 - y) + 1 - k
    lead0, lead1 = 3 * y, y + 1
    at_home = u == v

    def at(ref, r, c):
        return ref.at[
            pl.ds(pl.multiple_of(r * rows, rows), rows), pl.ds(pl.multiple_of(c * step, step), step)
        ]

    def copy(src, dst, ssem, rsem, dev):
        return pltpu.make_async_remote_copy(
            src_ref=src, dst_ref=dst, send_sem=ssem, recv_sem=rsem, device_id=(g, dev[0], dev[1]), device_id_type=MESH
        )

    to_sib, to_opp = (sib, z), (opp, z)
    up0, up1 = (lead0, z + dz), (lead1, z + dz)
    down1, down_same = (lead1, z - dz), (b, z - dz)
    across = (3 * (1 - y), z)

    def go(kind, c, src, ref, rsem, r, dev):
        copy(src, at(ref, r, c), send.at[kind, c], rsem.at[r, c], dev).start()

    def arrived(ref, rsem, r, c):
        copy(at(ref, r, c), at(ref, r, c), send.at[0, c], rsem.at[r, c], to_sib).wait_recv()

    hop0 = (u == 0) & ((v == 1) | (v == 2))
    hop1 = (u == 1) & (v == 2)
    lift = (v == 1) & (u == 1)

    barrier = pltpu.get_barrier_semaphore()
    for i in range(16):
        bb, zz = i // 4, i % 4

        @pl.when((bb != b) | (zz != z))
        def _():
            pl.semaphore_signal(barrier, inc=1, device_id=(g, bb, zz), device_id_type=MESH)

    pl.semaphore_wait(barrier, 15)

    def line_own(c):
        src = at(x, 0, c)
        pl.when(v == 1)(lambda: go(UP, c, src, xb, rb, own, up1))
        pl.when((v == 1) & (c < HELD))(lambda: go(DOWN, c, src, xb, rb, own, down1))

    line_own(0)
    line_own(1)

    @pl.loop(0, CHUNKS)
    def _(c):
        src = at(x, 0, c)
        go(TO_OPP, c, src, xz, rz, own, to_opp)
        pl.when(v == 0)(lambda: go(UP, c, src, xb, rb, own, up0))
        pl.when(v == 3)(lambda: go(DOWN, c, src, tr, rt, 0, down_same))
        go(TO_SIB, c, src, xz, rz, own, to_sib)

    def hop(kind, r, c, dev):
        arrived(xb, rb, r, c)
        go(kind, c, at(xb, r, c), xb, rb, r, dev)

    def end_waits(n):
        for i in range(CHUNKS // UNITS):
            c = n * (CHUNKS // UNITS) + i
            for r in (own, sib):
                pl.when(jnp.logical_not(at_home | hop0 | hop1))(lambda: arrived(xb, rb, r, c))
            for r in (opp, dia):
                pl.when(jnp.logical_not(at_home | hop1))(lambda: arrived(xb, rb, r, c))

    def stage_load(src):
        return pltpu.make_async_copy(src, stage, stage_sem.at[0])

    def band(ref, r):
        return ref.at[pl.ds(pl.multiple_of(r * rows, rows), rows)]

    @pl.loop(0, TICKS)
    def _(t):
        m, phase = t // 3, lax.rem(t, 3)

        @pl.when((t + 2 < CHUNKS) & (t >= 0))
        def _():
            line_own(t + 2)

        @pl.when(t < CHUNKS)
        def _():
            arrived(xz, rz, opp, t)
            src = at(xz, opp, t)
            pl.when(lift)(lambda: go(UP_OPP, t, src, xb, rb, opp, up1))
            pl.when((v == 1) & (t < HELD))(lambda: go(DOWN_OPP, t, src, xb, rb, opp, down1))
            go(FWD, t, src, xz, rz, opp, to_sib)

            @pl.when((u == 0) & (v == 1))
            def _():
                hop(HOP_OWN, own, t, up0)
                hop(HOP_SIB, sib, t, up0)

        @pl.when((t >= 1) & (t < CHUNKS + 1))
        def _():
            arrived(xz, rz, dia, t - 1)
            pl.when(lift)(lambda: go(UP_DIA, t - 1, at(xz, dia, t - 1), xb, rb, dia, up1))

        held = HELD + t - (CHUNKS + 2)

        @pl.when((v == 1) & (held >= HELD) & (held < CHUNKS))
        def _():
            go(DOWN, held, at(x, 0, held), xb, rb, own, down1)
            go(DOWN_OPP, held, at(xz, opp, held), xb, rb, opp, down1)

        slow, burst = m - 2, t - 2 * HELD
        late = jnp.where(v == 0, jnp.where(burst >= HELD - 3, burst, slow), t - 2 + v)
        paced = (v > 0) | ((phase == 1) & (slow < HELD - 3)) | (burst >= HELD - 3)

        @pl.when((v <= 2) & paced & (late >= 0) & (late < CHUNKS))
        def _():
            arrived(tr, rt, 0, late)
            src = at(tr, 0, late)
            pl.when(v >= 1)(lambda: go(PASS, late, src, tr, rt, 0, down_same))
            go(CROSS, late, src, xb, rb, own, across)

        @pl.when(hop1)
        def _():
            @pl.when((phase == 0) & (m >= 2) & (m < CHUNKS + 2))
            def _():
                hop(HOP_DIA, dia, m - 2, up1)

            @pl.when(t < 2)
            def _():
                hop(HOP_OWN, own, t, up1)
                hop(HOP_SIB, sib, t, up1)

            @pl.when((phase == 1) & (m < CHUNKS - 2))
            def _():
                hop(HOP_OWN, own, m + 2, up1)

            @pl.when((phase == 2) & (m < CHUNKS - 2))
            def _():
                hop(HOP_SIB, sib, m + 2, up1)

            @pl.when((phase == 2) & (m < CHUNKS))
            def _():
                hop(HOP_OPP, opp, m, up1)

        @pl.when((u == 0) & (v == 2) & (m >= 1) & (m <= CHUNKS))
        def _():
            pl.when(phase == 0)(lambda: hop(HOP_OWN, own, m - 1, up0))
            pl.when(phase == 1)(lambda: hop(HOP_SIB, sib, m - 1, up0))

        @pl.when(t == 9)
        def _():
            @pl.loop(0, CHUNKS)
            def _(c):
                arrived(xz, rz, sib, c)

        fill = (t == 3) | (t == 10) | (t == CHUNKS + 1) | (t == CHUNKS + 2)

        @pl.when(fill)
        def _():
            r = jnp.where(t == 3, own, jnp.where(t == 10, sib, jnp.where(t == CHUNKS + 1, opp, dia)))
            stage_load(x).wait()
            scale = wt[:, pl.ds(pl.multiple_of(r * rows, rows), rows)]

            @pl.loop(0, TILES)
            def _(i):
                p = pl.ds(pl.multiple_of(i * tile, tile), tile)
                turned = stage[:, p].T.astype(jnp.float32) * scale
                lhs[p, pl.ds(pl.multiple_of(r * rows, rows), rows)] = turned.astype(jnp.bfloat16)

        pl.when(t == 1)(lambda: stage_load(x).start())
        pl.when(t == 9)(lambda: stage_load(band(xz, sib)).start())
        pl.when(t == CHUNKS)(lambda: stage_load(band(xz, opp)).start())
        pl.when(t == CHUNKS + 1)(lambda: stage_load(band(xz, dia)).start())

        work = t - FIRST
        n, q = work // SPAN, lax.rem(work, SPAN)

        @pl.when((work >= 0) & (work < SPAN * EARLY))
        def _():
            s = lax.rem(n, 2)

            @pl.when(q == 0)
            def _():
                await_columns(xb, rhs.at[s], rhs_sem.at[s], rows, width)

            for j in range(PER_TICK):
                p = PER_TICK * q + j
                got = jnp.dot(
                    lhs[pl.ds(pl.multiple_of(p * tile, tile), tile), :], rhs[s], preferred_element_type=jnp.float32
                )
                kept[
                    pl.ds(pl.multiple_of(p * tile, tile), tile), pl.ds(pl.multiple_of(n * width, width), width)
                ] = got.astype(jnp.bfloat16)

        ahead = work + 1
        n_ahead = ahead // SPAN

        @pl.when((ahead >= 0) & (ahead < SPAN * EARLY) & (lax.rem(ahead, SPAN) == 0))
        def _():
            end_waits(n_ahead)
            s = lax.rem(n_ahead, 2)
            load_columns(x, xz, xb, rhs.at[s], rhs_sem.at[s], at_home, own, n_ahead, width)

    @pl.loop(EARLY, UNITS)
    def _(n):
        end_waits(n)

    sends = [
        (TO_SIB, True), (TO_OPP, True), (FWD, True),
        (UP, v <= 1), (DOWN, (v == 1) | (v == 3)), (DOWN_OPP, v == 1),
        (UP_OPP, lift), (UP_DIA, lift),
        (HOP_OWN, hop0 | hop1), (HOP_SIB, hop0 | hop1), (HOP_OPP, hop1), (HOP_DIA, hop1),
        (PASS, (v == 1) | (v == 2)), (CROSS, v <= 2),
    ]

    @pl.loop(0, CHUNKS)
    def _(c):
        for kind, cond in sends:
            when(cond, lambda: copy(at(x, 0, c), at(xz, 0, c), send.at[kind, c], rz.at[0, c], to_sib).wait_send())


def gather(pair_block, weights):
    rows, cols = pair_block.shape
    width = cols // UNITS
    bf16 = jnp.bfloat16
    full = jax.ShapeDtypeStruct((4 * rows, cols), bf16)
    return pl.pallas_call(
        gather_kernel,
        out_shape=(
            full,
            full,
            jax.ShapeDtypeStruct((rows, cols), bf16),
            pltpu.VMEM((cols, 4 * rows), bf16),
            pltpu.VMEM((cols, EARLY * width), bf16),
        ),
        in_specs=[pl.BlockSpec(memory_space=pl.ANY), pl.BlockSpec(memory_space=pltpu.VMEM)],
        out_specs=[pl.BlockSpec(memory_space=m) for m in (pltpu.HBM,) * 3 + (pltpu.VMEM,) * 2],
        scratch_shapes=[
            pltpu.VMEM((rows, cols), bf16),
            pltpu.VMEM((2, 4 * rows, width), bf16),
            pltpu.SemaphoreType.DMA((14, CHUNKS)),
            pltpu.SemaphoreType.DMA((4, CHUNKS)),
            pltpu.SemaphoreType.DMA((4, CHUNKS)),
            pltpu.SemaphoreType.DMA((1, CHUNKS)),
            pltpu.SemaphoreType.DMA((1,)),
            pltpu.SemaphoreType.DMA((2, 4)),
        ],
        compiler_params=pltpu.CompilerParams(collective_id=0, has_side_effects=True, vmem_limit_bytes=13 * MIB),
    )(pair_block, weights[None, :])


def finish_kernel(x, xz, xb, lhs, kept, out, rhs, acc, hold, rhs_sem, acc_sem, out_sem):
    rows, cols = x.shape
    width, tile = cols // UNITS, cols // TILES
    strip = tile // STRIPS
    done = EARLY * width
    b, z, y, k, u, v = place()

    def span(i, size):
        return pl.ds(pl.multiple_of(i * size, size), size)

    def put(i):
        s = lax.rem(i, SLOTS)
        return pltpu.make_async_copy(hold.at[s], out.at[span(i, strip), pl.ds(0, done)], out_sem.at[s])

    def store(p):
        s = lax.rem(p, 2)
        return pltpu.make_async_copy(acc.at[s], out.at[span(p, tile), pl.ds(done, width)], acc_sem.at[s])

    load_columns(x, xz, xb, rhs, rhs_sem, u == v, b, EARLY, width)

    @pl.loop(0, TILES)
    def _(p):
        for j in range(STRIPS):
            i = p * STRIPS + j
            pl.when(i >= SLOTS)(lambda: put(i - SLOTS).wait())
            hold[lax.rem(i, SLOTS)] = kept[span(i, strip), :].astype(jnp.float32)
            put(i).start()
        pl.when(p == 0)(lambda: await_columns(xb, rhs, rhs_sem, rows, width))
        pl.when(p >= 2)(lambda: store(p - 2).wait())
        acc[lax.rem(p, 2)] = jnp.dot(lhs[span(p, tile), :], rhs[...], preferred_element_type=jnp.float32)
        store(p).start()

    for p in range(TILES - 2, TILES):
        store(p).wait()
    for i in range(TILES * STRIPS - SLOTS, TILES * STRIPS):
        put(i).wait()


def finish(pair_block, xz, xb, lhs, kept):
    rows, cols = pair_block.shape
    width, tile = cols // UNITS, cols // TILES
    bf16, f32 = jnp.bfloat16, jnp.float32
    lhs = pltpu.with_memory_space_constraint(lhs, pltpu.VMEM)
    kept = pltpu.with_memory_space_constraint(kept, pltpu.VMEM)
    return pl.pallas_call(
        finish_kernel,
        out_shape=jax.ShapeDtypeStruct((cols, cols), f32),
        in_specs=[pl.BlockSpec(memory_space=m) for m in (pl.ANY,) * 3 + (pltpu.VMEM,) * 2],
        out_specs=pl.BlockSpec(memory_space=pl.ANY),
        scratch_shapes=[
            pltpu.VMEM((4 * rows, width), bf16),
            pltpu.VMEM((2, tile, width), f32),
            pltpu.VMEM((SLOTS, tile // STRIPS, EARLY * width), f32),
            pltpu.SemaphoreType.DMA((4,)),
            pltpu.SemaphoreType.DMA((2,)),
            pltpu.SemaphoreType.DMA((SLOTS,)),
        ],
        compiler_params=pltpu.CompilerParams(vmem_limit_bytes=17 * MIB),
    )(pair_block, xz, xb, lhs, kept)


def shards(square, pair_block, occ_energy, virt_energy, frequency):
    weights = pair_weights(occ_energy, virt_energy, frequency)
    if square:
        xz, xb, _, lhs, kept = gather(pair_block, weights)
        return finish(pair_block, xz, xb, lhs, kept)
    row_full = lax.all_gather(pair_block, "col", axis=1, tiled=True)
    column_slab = lax.all_to_all(row_full, "blk", split_axis=1, concat_axis=0, tiled=True)
    own_columns = lax.all_gather(pair_block, "blk", axis=0, tiled=True)
    scaled = (own_columns.astype(jnp.float32) * weights[:, None]).astype(jnp.bfloat16)
    return lax.dot_general(
        scaled, column_slab, (((0,), (0,)), ((), ())), preferred_element_type=jnp.float32
    )


def solution(mesh):
    square = mesh.shape["blk"] == 4 and mesh.shape["col"] == 4
    return jax.shard_map(
        functools.partial(shards, square),
        mesh=mesh,
        in_specs=(P(("groups", "blk"), "col"), P("groups"), P("groups"), P("groups")),
        out_specs=P(("groups", "col"), "blk"),
        check_vma=False,
    )
```

time: 344 us -> 316 us (0.919)
  Pallas kernels: 336 us -> 310 us
    pallas_call x1, Pallas kernels: 49 us -> 22.9 us  [finish(): pl.pallas_call(finish_kernel, out_shape=jax.ShapeDtypeStruct((cols, cols)...]
where the time goes in v2:
time: 316 us; the launch traced here: 312 us
  Pallas kernels  310 us (98%)
    pallas_call x1, Pallas kernels, gather(): pl.pallas_call(gather_kernel, out_shape=(full, full, jax.ShapeDtypeStruct...  287 us
    pallas_call x1, Pallas kernels, finish(): pl.pallas_call(finish_kernel, out_shape=jax.ShapeDtypeStruct((cols, cols)...  22.9 us

profile of v2, /device:TPU:16, one launch (start us, length us, event | category | flops | bytes accessed | tf_op | source)
XLA Modules:
  0.0 312.2 jit_solution(1500124199057689091)
XLA Ops:
  1.3 1.3 add_divide_fusion
  2.6 286.7 %shard_map.46 = (bf16[2048,4096]{1,0:T(8,128)(2,1)}, bf16[2048,4096]{1,0:T(8,128)(2,1)}, bf16[512,4096]{1,0:T(8,128)(2,1)}, bf16[4096,2048]{1,0:T(8,128)(2,1)S(1)}, bf16[4096,3584]{1,0:T(8,128)(2,1)S(1)}) custom-call(bf16[512,4096]{1,0:T(8,128)(2,1)} %x.3, f32[1,2048]{1,0:T(1,128)} %bitcast.4), custom_call_target="tpu_custom_call" | custom-call | tf_op jit(solution)/shard_map/pallas_call | solution.py:308
  289.3 22.9 %shard_map.47 = f32[4096,4096]{1,0:T(8,128)} custom-call(bf16[512,4096]{1,0:T(8,128)(2,1)} %x.3, bf16[2048,4096]{1,0:T(8,128)(2,1)} %get-tuple-element.9.xz, bf16[2048,4096]{1,0:T(8,128)(2,1)} %get-tuple-element.10.xb, bf16[4096,2048]{1,0:T(8,128)(2,1)S(1)} %get-tuple-element.11.lhs, bf16[4096,3584]{1,0:T(8,128)(2,1)S(1)} %get-tuple-element.12.kept), custom_call_target="tpu_custom_call" | custom-call | tf_op jit(solution)/shard_map/pallas_call | solution.py:377

commit v3 on v2

--- a/solution.py
+++ b/solution.py
@@ -9,18 +9,24 @@
 
 MESH = pl.DeviceIdType.MESH
 CHUNKS = 32
-UNITS = 8
+UNITS = 16
 TILES = 8
-EARLY = 7
+EARLY = 13
 FIRST = CHUNKS + 11
 HELD = 3 * CHUNKS // 4
 TICKS = 3 * CHUNKS + 4
-PER_TICK = 32 // CHUNKS
+PER_TICK = 64 // CHUNKS
 SPAN = TILES // PER_TICK
 MIB = 1 << 20
-TO_SIB, TO_OPP, UP, DOWN, FWD, DOWN_OPP, UP_OPP, UP_DIA, HOP_OWN, HOP_SIB, HOP_OPP, HOP_DIA, PASS, CROSS = range(14)
+TAIL = CHUNKS // 16
+CUT = CHUNKS - TAIL
+TO_SIB, TO_OPP, UP, DOWN, FWD, DOWN_OPP, UP_OPP, UP_DIA, HOP_OWN, HOP_SIB, HOP_OPP, HOP_DIA, PASS, CROSS, SIDE, SIDE_CROSS = range(16)
 SLOTS = 6
 STRIPS = 4
+
+
+def aside(c):
+    return (c >= CUT - 7) & (c < CUT - 1)
 
 
 def pair_weights(occ_energy, virt_energy, frequency):
@@ -36,16 +42,9 @@
     return b, z, y, k, u, v
 
 
-def when(cond, f):
-    if cond is True:
-        f()
-    else:
-        pl.when(cond)(f)
-
-
-def load_columns(x, xz, xb, dst, sem, at_home, own, n, width):
+def load_columns(x, xz, xb, dst, sem, at_home, own, n, width, count=1):
     rows = x.shape[0]
-    cols = pl.ds(pl.multiple_of(n * width, width), width)
+    cols = pl.ds(pl.multiple_of(n * width, width), count * width)
 
     def piece(src, r):
         return pltpu.make_async_copy(src, dst.at[pl.ds(pl.multiple_of(r * rows, rows), rows)], sem.at[r])
@@ -73,8 +72,8 @@
 
 
 def gather_kernel(
-    x, wt, xz, xb, tr, lhs, kept,
-    stage, rhs, send, rz, rb, rt, stage_sem, rhs_sem,
+    x, occ, virt, freq, xz, xb, tr, ts, tail_h, tail_o, lhs_out, lhs, kept,
+    stage, rhs, wt, send, rz, rb, rt, rs, stage_sem, rhs_sem, tail_sem, lhs_sem,
 ):
     rows, cols = x.shape
     step = cols // CHUNKS
@@ -103,28 +102,52 @@
     across = (3 * (1 - y), z)
 
     def go(kind, c, src, ref, rsem, r, dev):
-        copy(src, at(ref, r, c), send.at[kind, c], rsem.at[r, c], dev).start()
+        copy(src, at(ref, r, c), send.at[kind], rsem.at[r, c], dev).start()
 
     def arrived(ref, rsem, r, c):
-        copy(at(ref, r, c), at(ref, r, c), send.at[0, c], rsem.at[r, c], to_sib).wait_recv()
+        copy(at(ref, r, c), at(ref, r, c), send.at[0], rsem.at[r, c], to_sib).wait_recv()
 
     hop0 = (u == 0) & ((v == 1) | (v == 2))
     hop1 = (u == 1) & (v == 2)
     lift = (v == 1) & (u == 1)
 
     barrier = pltpu.get_barrier_semaphore()
-    for i in range(16):
-        bb, zz = i // 4, i % 4
-
-        @pl.when((bb != b) | (zz != z))
-        def _():
-            pl.semaphore_signal(barrier, inc=1, device_id=(g, bb, zz), device_id_type=MESH)
-
-    pl.semaphore_wait(barrier, 15)
+    last = lax.axis_size("col") - 1
+
+    def greet(dev):
+        pl.semaphore_signal(barrier, inc=1, device_id=(g,) + dev, device_id_type=MESH)
+
+    for dev in ((sib, z), (opp, z), (dia, z)):
+        greet(dev)
+    for core in (own, sib):
+        pl.when(z > 0)(lambda: greet((core, z - 1)))
+        pl.when(z < last)(lambda: greet((core, z + 1)))
+    pl.semaphore_wait(barrier, 3 + 2 * (z > 0).astype(jnp.int32) + 2 * (z < last).astype(jnp.int32))
+
+    homes = [(own, tail_h, k), (sib, tail_h, 1 - k), (opp, tail_o, k), (dia, tail_o, 1 - k)]
+
+    def tail_at(r, c):
+        ref, i = next((ref, i) for key, ref, i in homes if key is r)
+        return ref.at[
+            pl.ds(pl.multiple_of(i * rows, rows), rows), pl.ds(pl.multiple_of((c - CUT) * step, step), step)
+        ]
+
+    def go_xb(kind, c, src, r, dev):
+        def main():
+            copy(src, at(xb, r, c), send.at[kind], rb.at[r, c], dev).start()
+
+        def tail():
+            copy(src, tail_at(r, c), send.at[kind], rb.at[r, c], dev).start()
+
+        if isinstance(c, int):
+            main()
+        else:
+            pl.when(c < CUT)(main)
+            pl.when(c >= CUT)(tail)
 
     def line_own(c):
         src = at(x, 0, c)
-        pl.when(v == 1)(lambda: go(UP, c, src, xb, rb, own, up1))
+        pl.when(v == 1)(lambda: go_xb(UP, c, src, own, up1))
         pl.when((v == 1) & (c < HELD))(lambda: go(DOWN, c, src, xb, rb, own, down1))
 
     line_own(0)
@@ -134,27 +157,54 @@
     def _(c):
         src = at(x, 0, c)
         go(TO_OPP, c, src, xz, rz, own, to_opp)
-        pl.when(v == 0)(lambda: go(UP, c, src, xb, rb, own, up0))
+        pl.when(v == 0)(lambda: go_xb(UP, c, src, own, up0))
         pl.when(v == 3)(lambda: go(DOWN, c, src, tr, rt, 0, down_same))
         go(TO_SIB, c, src, xz, rz, own, to_sib)
 
     def hop(kind, r, c, dev):
         arrived(xb, rb, r, c)
-        go(kind, c, at(xb, r, c), xb, rb, r, dev)
+
+        @pl.when(c < CUT)
+        def _():
+            go(kind, c, at(xb, r, c), xb, rb, r, dev)
+
+        @pl.when((c >= CUT) & (v == 1))
+        def _():
+            go_tail = copy(tail_at(r, c), tail_at(r, c), send.at[kind], rb.at[r, c], dev)
+            go_tail.start()
 
     def end_waits(n):
         for i in range(CHUNKS // UNITS):
             c = n * (CHUNKS // UNITS) + i
             for r in (own, sib):
-                pl.when(jnp.logical_not(at_home | hop0 | hop1))(lambda: arrived(xb, rb, r, c))
+                pl.when(jnp.logical_not(at_home | hop0 | hop1) & (c < CUT))(lambda: arrived(xb, rb, r, c))
             for r in (opp, dia):
-                pl.when(jnp.logical_not(at_home | hop1))(lambda: arrived(xb, rb, r, c))
+                pl.when(jnp.logical_not(at_home | hop1) & ((c < CUT) | (u == 0)))(lambda: arrived(xb, rb, r, c))
 
     def stage_load(src):
         return pltpu.make_async_copy(src, stage, stage_sem.at[0])
 
     def band(ref, r):
         return ref.at[pl.ds(pl.multiple_of(r * rows, rows), rows)]
+
+    def go_across(kind, c, src, dev):
+        @pl.when(c < CUT)
+        def _():
+            go(kind, c, src, xb, rb, own, dev)
+
+        @pl.when(c >= CUT)
+        def _():
+            copy(src, tail_at(opp, c), send.at[kind], rb.at[own, c], dev).start()
+
+    def rest(ref, half):
+        r = pl.ds(pl.multiple_of(half * 2 * rows, 2 * rows), 2 * rows)
+        return rhs.at[0, r, pl.ds(0, TAIL * step)]
+
+    lhs_save = pltpu.make_async_copy(lhs, lhs_out, lhs_sem.at[0])
+
+    for i in range(occ.shape[0]):
+        gap = virt[...] - occ[i]
+        wt[:, pl.ds(i * virt.shape[1], virt.shape[1])] = 2.0 * gap / (gap * gap + freq[0] * freq[0])
 
     @pl.loop(0, TICKS)
     def _(t):
@@ -168,7 +218,7 @@
         def _():
             arrived(xz, rz, opp, t)
             src = at(xz, opp, t)
-            pl.when(lift)(lambda: go(UP_OPP, t, src, xb, rb, opp, up1))
+            pl.when(lift & jnp.logical_not(aside(t)))(lambda: go_xb(UP_OPP, t, src, opp, up1))
             pl.when((v == 1) & (t < HELD))(lambda: go(DOWN_OPP, t, src, xb, rb, opp, down1))
             go(FWD, t, src, xz, rz, opp, to_sib)
 
@@ -180,11 +230,14 @@
         @pl.when((t >= 1) & (t < CHUNKS + 1))
         def _():
             arrived(xz, rz, dia, t - 1)
-            pl.when(lift)(lambda: go(UP_DIA, t - 1, at(xz, dia, t - 1), xb, rb, dia, up1))
+
+            @pl.when(lift & jnp.logical_not(aside(t - 1)))
+            def _():
+                go_xb(UP_DIA, t - 1, at(xz, dia, t - 1), dia, up1)
 
         held = HELD + t - (CHUNKS + 2)
 
-        @pl.when((v == 1) & (held >= HELD) & (held < CHUNKS))
+        @pl.when((v == 1) & (held >= HELD) & (held < CUT))
         def _():
             go(DOWN, held, at(x, 0, held), xb, rb, own, down1)
             go(DOWN_OPP, held, at(xz, opp, held), xb, rb, opp, down1)
@@ -198,7 +251,20 @@
             arrived(tr, rt, 0, late)
             src = at(tr, 0, late)
             pl.when(v >= 1)(lambda: go(PASS, late, src, tr, rt, 0, down_same))
-            go(CROSS, late, src, xb, rb, own, across)
+            go_across(CROSS, late, src, across)
+
+        @pl.when((v == 2) & (t == CHUNKS // 2))
+        def _():
+            @pl.loop(0, CHUNKS)
+            def _(c):
+                pl.when(aside(c))(lambda: go(SIDE, c, at(x, 0, c), ts, rs, 0, down_same))
+
+        side = t - (CHUNKS + 2) + CUT - 7
+
+        @pl.when((v == 1) & (t >= CHUNKS + 2) & aside(side))
+        def _():
+            arrived(ts, rs, 0, side)
+            go(SIDE_CROSS, side, at(ts, 0, side), xb, rb, own, (2 - y, z))
 
         @pl.when(hop1)
         def _():
@@ -233,6 +299,20 @@
             @pl.loop(0, CHUNKS)
             def _(c):
                 arrived(xz, rz, sib, c)
+
+        @pl.when(at_home & (t == CHUNKS + 5))
+        def _():
+            near = rhs.at[0, :, pl.ds(0, TAIL * step)]
+            load_columns(x, xz, xb, near, rhs_sem.at[0], at_home, own, CUT // TAIL, TAIL * step)
+            await_columns(xb, near, rhs_sem.at[0], rows, TAIL * step)
+            saves = [
+                pltpu.make_async_copy(rest(tail_h, y), tail_h, tail_sem.at[0]),
+                pltpu.make_async_copy(rest(tail_o, 1 - y), tail_o, tail_sem.at[1]),
+            ]
+            for save in saves:
+                save.start()
+            for save in saves:
+                save.wait()
 
         fill = (t == 3) | (t == 10) | (t == CHUNKS + 1) | (t == CHUNKS + 2)
 
@@ -248,6 +328,7 @@
                 turned = stage[:, p].T.astype(jnp.float32) * scale
                 lhs[p, pl.ds(pl.multiple_of(r * rows, rows), rows)] = turned.astype(jnp.bfloat16)
 
+        pl.when(t == CHUNKS + 3)(lambda: lhs_save.start())
         pl.when(t == 1)(lambda: stage_load(x).start())
         pl.when(t == 9)(lambda: stage_load(band(xz, sib)).start())
         pl.when(t == CHUNKS)(lambda: stage_load(band(xz, opp)).start())
@@ -282,63 +363,87 @@
             s = lax.rem(n_ahead, 2)
             load_columns(x, xz, xb, rhs.at[s], rhs_sem.at[s], at_home, own, n_ahead, width)
 
-    @pl.loop(EARLY, UNITS)
-    def _(n):
-        end_waits(n)
-
-    sends = [
-        (TO_SIB, True), (TO_OPP, True), (FWD, True),
-        (UP, v <= 1), (DOWN, (v == 1) | (v == 3)), (DOWN_OPP, v == 1),
-        (UP_OPP, lift), (UP_DIA, lift),
-        (HOP_OWN, hop0 | hop1), (HOP_SIB, hop0 | hop1), (HOP_OPP, hop1), (HOP_DIA, hop1),
-        (PASS, (v == 1) | (v == 2)), (CROSS, v <= 2),
-    ]
-
-    @pl.loop(0, CHUNKS)
-    def _(c):
-        for kind, cond in sends:
-            when(cond, lambda: copy(at(x, 0, c), at(xz, 0, c), send.at[kind, c], rz.at[0, c], to_sib).wait_send())
-
-
-def gather(pair_block, weights):
+    def drain(kind, count):
+        sent = x.at[:, pl.ds(0, count * step)]
+        copy(sent, sent, send.at[kind], rz.at[0, 0], to_sib).wait_send()
+
+    def drain_if(cond, kind, count):
+        pl.when(cond)(lambda: drain(kind, count))
+
+    def finals():
+        @pl.loop(EARLY, UNITS)
+        def _(n):
+            end_waits(n)
+
+    few = CUT - 1 - (CUT - 7)
+    lhs_save.wait()
+    for kind in (TO_SIB, TO_OPP, FWD):
+        drain(kind, CHUNKS)
+    drain_if(v == 2, SIDE, few)
+    drain_if(v == 1, SIDE_CROSS, few)
+    drain_if(v <= 2, CROSS, CHUNKS)
+    drain_if((v == 1) | (v == 2), PASS, CHUNKS)
+    drain_if(v == 0, UP, CHUNKS)
+    drain_if(v == 3, DOWN, CHUNKS)
+    finals()
+    drain_if(v == 1, UP, CHUNKS)
+    for kind in (UP_OPP, UP_DIA):
+        drain_if(lift, kind, CHUNKS - few)
+    for kind in (DOWN, DOWN_OPP):
+        drain_if(v == 1, kind, CUT)
+    for kind in (HOP_OWN, HOP_SIB):
+        drain_if((u == 0) & (v == 1), kind, CHUNKS)
+        drain_if(v == 2, kind, CUT)
+    for kind in (HOP_OPP, HOP_DIA):
+        drain_if(hop1, kind, CUT)
+
+
+def gather(pair_block, occ_energy, virt_energy, frequency):
     rows, cols = pair_block.shape
-    width = cols // UNITS
+    width, narrow = cols // UNITS, cols * TAIL // CHUNKS
     bf16 = jnp.bfloat16
     full = jax.ShapeDtypeStruct((4 * rows, cols), bf16)
+    block = jax.ShapeDtypeStruct((rows, cols), bf16)
+    half = jax.ShapeDtypeStruct((2 * rows, narrow), bf16)
     return pl.pallas_call(
         gather_kernel,
         out_shape=(
-            full,
-            full,
-            jax.ShapeDtypeStruct((rows, cols), bf16),
+            full, full, block, block, half, half,
+            jax.ShapeDtypeStruct((cols, 4 * rows), bf16),
             pltpu.VMEM((cols, 4 * rows), bf16),
             pltpu.VMEM((cols, EARLY * width), bf16),
         ),
-        in_specs=[pl.BlockSpec(memory_space=pl.ANY), pl.BlockSpec(memory_space=pltpu.VMEM)],
-        out_specs=[pl.BlockSpec(memory_space=m) for m in (pltpu.HBM,) * 3 + (pltpu.VMEM,) * 2],
+        in_specs=[pl.BlockSpec(memory_space=m) for m in (pl.ANY, pltpu.SMEM, pltpu.VMEM, pltpu.SMEM)],
+        out_specs=[pl.BlockSpec(memory_space=m) for m in (pltpu.HBM,) * 7 + (pltpu.VMEM,) * 2],
         scratch_shapes=[
             pltpu.VMEM((rows, cols), bf16),
             pltpu.VMEM((2, 4 * rows, width), bf16),
-            pltpu.SemaphoreType.DMA((14, CHUNKS)),
+            pltpu.VMEM((1, 4 * rows), jnp.float32),
+            pltpu.SemaphoreType.DMA((16,)),
             pltpu.SemaphoreType.DMA((4, CHUNKS)),
             pltpu.SemaphoreType.DMA((4, CHUNKS)),
             pltpu.SemaphoreType.DMA((1, CHUNKS)),
+            pltpu.SemaphoreType.DMA((1, CHUNKS)),
             pltpu.SemaphoreType.DMA((1,)),
             pltpu.SemaphoreType.DMA((2, 4)),
+            pltpu.SemaphoreType.DMA((2,)),
+            pltpu.SemaphoreType.DMA((1,)),
         ],
         compiler_params=pltpu.CompilerParams(collective_id=0, has_side_effects=True, vmem_limit_bytes=13 * MIB),
-    )(pair_block, weights[None, :])
+    )(pair_block, occ_energy, virt_energy[None, :], frequency)
+
+
+def span(i, size):
+    return pl.ds(pl.multiple_of(i * size, size), size)
 
 
 def finish_kernel(x, xz, xb, lhs, kept, out, rhs, acc, hold, rhs_sem, acc_sem, out_sem):
     rows, cols = x.shape
-    width, tile = cols // UNITS, cols // TILES
+    width, tile, narrow = cols // UNITS, cols // TILES, cols * TAIL // CHUNKS
     strip = tile // STRIPS
     done = EARLY * width
+    mid = cols - narrow - done
     b, z, y, k, u, v = place()
-
-    def span(i, size):
-        return pl.ds(pl.multiple_of(i * size, size), size)
 
     def put(i):
         s = lax.rem(i, SLOTS)
@@ -346,9 +451,10 @@
 
     def store(p):
         s = lax.rem(p, 2)
-        return pltpu.make_async_copy(acc.at[s], out.at[span(p, tile), pl.ds(done, width)], acc_sem.at[s])
-
-    load_columns(x, xz, xb, rhs, rhs_sem, u == v, b, EARLY, width)
+        cut = pl.ds(done, mid)
+        return pltpu.make_async_copy(acc.at[s], out.at[span(p, tile), cut], acc_sem.at[s])
+
+    load_columns(x, xz, xb, rhs, rhs_sem, u == v, b, EARLY, width, mid // width)
 
     @pl.loop(0, TILES)
     def _(p):
@@ -357,7 +463,7 @@
             pl.when(i >= SLOTS)(lambda: put(i - SLOTS).wait())
             hold[lax.rem(i, SLOTS)] = kept[span(i, strip), :].astype(jnp.float32)
             put(i).start()
-        pl.when(p == 0)(lambda: await_columns(xb, rhs, rhs_sem, rows, width))
+        pl.when(p == 0)(lambda: await_columns(xb, rhs, rhs_sem, rows, mid))
         pl.when(p >= 2)(lambda: store(p - 2).wait())
         acc[lax.rem(p, 2)] = jnp.dot(lhs[span(p, tile), :], rhs[...], preferred_element_type=jnp.float32)
         store(p).start()
@@ -370,32 +476,117 @@
 
 def finish(pair_block, xz, xb, lhs, kept):
     rows, cols = pair_block.shape
-    width, tile = cols // UNITS, cols // TILES
+    width, tile, narrow = cols // UNITS, cols // TILES, cols * TAIL // CHUNKS
+    mid = cols - narrow - EARLY * width
     bf16, f32 = jnp.bfloat16, jnp.float32
-    lhs = pltpu.with_memory_space_constraint(lhs, pltpu.VMEM)
-    kept = pltpu.with_memory_space_constraint(kept, pltpu.VMEM)
     return pl.pallas_call(
         finish_kernel,
         out_shape=jax.ShapeDtypeStruct((cols, cols), f32),
         in_specs=[pl.BlockSpec(memory_space=m) for m in (pl.ANY,) * 3 + (pltpu.VMEM,) * 2],
         out_specs=pl.BlockSpec(memory_space=pl.ANY),
         scratch_shapes=[
-            pltpu.VMEM((4 * rows, width), bf16),
-            pltpu.VMEM((2, tile, width), f32),
+            pltpu.VMEM((4 * rows, mid), bf16),
+            pltpu.VMEM((2, tile, mid), f32),
             pltpu.VMEM((SLOTS, tile // STRIPS, EARLY * width), f32),
             pltpu.SemaphoreType.DMA((4,)),
             pltpu.SemaphoreType.DMA((2,)),
             pltpu.SemaphoreType.DMA((SLOTS,)),
         ],
-        compiler_params=pltpu.CompilerParams(vmem_limit_bytes=17 * MIB),
+        cost_estimate=pl.CostEstimate(flops=10**10, bytes_accessed=cols * cols * 4, transcendentals=0),
+        compiler_params=pltpu.CompilerParams(vmem_limit_bytes=16 * MIB),
     )(pair_block, xz, xb, lhs, kept)
 
 
-def shards(square, pair_block, occ_energy, virt_energy, frequency):
+def tail_kernel(lhs_in, tail_h, tail_o, got_h, got_o, _, out, lhs, rhs, acc, lhs_sem, rhs_sem, acc_sem):
+    cols = out.shape[0]
+    tile, narrow = cols // TILES, rhs.shape[1]
+    half = tail_h.shape[0]
+    b, z, y, k, u, v = place()
+    parts = [(tail_h, got_h, y, (v == 3) | ((v == 0) & (u == 1))), (tail_o, got_o, 1 - y, (u == 1) & ((v == 3) | (v == 0)))]
+
+    def fetch(src, at, i):
+        return pltpu.make_async_copy(src, rhs.at[pl.ds(pl.multiple_of(at * half, half), half)], rhs_sem.at[i])
+
+    def store(p):
+        s = lax.rem(p, 2)
+        return pltpu.make_async_copy(acc.at[s], out.at[span(p, tile), pl.ds(cols - narrow, narrow)], acc_sem.at[s])
+
+    def turn(p):
+        return pltpu.make_async_copy(lhs_in.at[span(p, tile)], lhs.at[lax.rem(p, 3)], lhs_sem.at[lax.rem(p, 3)])
+
+    turn(0).start()
+    for i, (near, far, at, remote) in enumerate(parts):
+        pl.when(remote)(lambda: fetch(far, at, i).start())
+        pl.when(jnp.logical_not(remote))(lambda: fetch(near, at, i).start())
+    turn(1).start()
+    for i, (near, far, at, remote) in enumerate(parts):
+        fetch(near, at, i).wait()
+
+    @pl.loop(0, TILES)
+    def _(p):
+        turn(p).wait()
+        pl.when(p + 2 < TILES)(lambda: turn(p + 2).start())
+        pl.when(p >= 2)(lambda: store(p - 2).wait())
+        acc[lax.rem(p, 2)] = jnp.dot(lhs[lax.rem(p, 3)], rhs[...], preferred_element_type=jnp.float32)
+        store(p).start()
+
+    for p in range(TILES - 2, TILES):
+        store(p).wait()
+
+
+def close(lhs, tail_h, tail_o, got_h, got_o, out):
+    cols, depth = lhs.shape
+    tile, narrow = cols // TILES, tail_h.shape[1]
+    return pl.pallas_call(
+        tail_kernel,
+        out_shape=jax.ShapeDtypeStruct(out.shape, out.dtype),
+        in_specs=[pl.BlockSpec(memory_space=m) for m in (pl.ANY,) * 6],
+        out_specs=pl.BlockSpec(memory_space=pl.ANY),
+        scratch_shapes=[
+            pltpu.VMEM((3, tile, depth), jnp.bfloat16),
+            pltpu.VMEM((depth, narrow), jnp.bfloat16),
+            pltpu.VMEM((2, tile, narrow), jnp.float32),
+            pltpu.SemaphoreType.DMA((3,)),
+            pltpu.SemaphoreType.DMA((2,)),
+            pltpu.SemaphoreType.DMA((2,)),
+        ],
+        input_output_aliases={5: 0},
+        compiler_params=pltpu.CompilerParams(vmem_limit_bytes=52 * MIB),
+    )(lhs, tail_h, tail_o, got_h, got_o, out)
+
+
+def last_hops(groups):
+    def index(g, b, z):
+        return (g * 4 + b) * 4 + z
+
+    both, lone = [], []
+    for i in range(groups * 16):
+        g, b, z = i // 16, i // 4 % 4, i % 4
+        y, k = b // 2, b % 2
+        u, v = k + y - 2 * y * k, z + y * (3 - 2 * z)
+        d = 1 - 2 * y
+        if v == 2:
+            both.append((i, index(g, b, z + d)))
+            if u == 1:
+                lone.append((i, index(g, b, z + d)))
+        if v == 1 and u == 1:
+            both.append((i, index(g, b, z - d)))
+            lone.append((i, index(g, b, z - d)))
+    return both, lone
+
+
+def shards(square, groups, pair_block, occ_energy, virt_energy, frequency):
+    if square:
+        xz, xb, _, _, tail_h, tail_o, lhs_back, lhs, kept = gather(pair_block, occ_energy, virt_energy, frequency)
+        both, lone = last_hops(groups)
+        axes = ("groups", "blk", "col")
+        got_h = lax.ppermute(tail_h, axes, both)
+        got_o = lax.ppermute(tail_o, axes, lone)
+        lhs = pltpu.with_memory_space_constraint(lhs, pltpu.VMEM)
+        kept = pltpu.with_memory_space_constraint(kept, pltpu.VMEM)
+        out = finish(pair_block, xz, xb, lhs, kept)
+        return close(lhs_back, tail_h, tail_o, got_h, got_o, out)
     weights = pair_weights(occ_energy, virt_energy, frequency)
-    if square:
-        xz, xb, _, lhs, kept = gather(pair_block, weights)
-        return finish(pair_block, xz, xb, lhs, kept)
     row_full = lax.all_gather(pair_block, "col", axis=1, tiled=True)
     column_slab = lax.all_to_all(row_full, "blk", split_axis=1, concat_axis=0, tiled=True)
     own_columns = lax.all_gather(pair_block, "blk", axis=0, tiled=True)
@@ -408,7 +599,7 @@
 def solution(mesh):
     square = mesh.shape["blk"] == 4 and mesh.shape["col"] == 4
     return jax.shard_map(
-        functools.partial(shards, square),
+        functools.partial(shards, square, mesh.shape["groups"]),
         mesh=mesh,
         in_specs=(P(("groups", "blk"), "col"), P("groups"), P("groups"), P("groups")),
         out_specs=P(("groups", "col"), "blk"),

time: 316 us -> 306 us (0.968)
  Pallas kernels: 310 us -> 296 us
  starting transfers between devices: 0 us -> 3.71 us
    pallas_call x1 -> x2, Pallas kernels: 287 us -> 274 us  [the longest x1 264 us: gather(): pl.pallas_call(gather_kernel, out_shape=(full, full, block, block, half,...]
    ppermute x0 -> x2, starting transfers between devices: none -> 3.71 us  [the longest x1 3.02 us: shards(): got_h = lax.ppermute(tail_h, axes, both)]
  transfers between devices with their start and end apart: 0 -> 2, of which waited for: 0 -> 0; matrix products, arithmetic and copies ran while one was open for 0% -> 0% of each run, Pallas kernels for 0% -> 7%
where the time goes in v3:
time: 306 us; the launch traced here: 302 us
  Pallas kernels  296 us (97%)
  starting transfers between devices  3.71 us (1%)
    pallas_call x1, Pallas kernels, gather(): pl.pallas_call(gather_kernel, out_shape=(full, full, block, block, half,...  264 us
    pallas_call x1, Pallas kernels, finish(): pl.pallas_call(finish_kernel, out_shape=jax.ShapeDtypeStruct((cols, cols)...  22.1 us
    pallas_call x1, Pallas kernels, close(): pl.pallas_call(tail_kernel, out_shape=jax.ShapeDtypeStruct(out.shape, out...  9.56 us
  transfers between devices with their start and end apart: 2, of which 0 were waited for; matrix products, arithmetic and copies ran while one was open for 0% of the time, Pallas kernels for 7%

profile of v3, /device:TPU:16, one launch (start us, length us, event | category | flops | bytes accessed | tf_op | source)
XLA Modules:
  0.0 301.9 jit_solution(14898532744043393298)
XLA Ops:
  1.3 264.4 %shard_map.46 = (bf16[2048,4096]{1,0:T(8,128)(2,1)}, bf16[2048,4096]{1,0:T(8,128)(2,1)}, bf16[512,4096]{1,0:T(8,128)(2,1)}, bf16[512,4096]{1,0:T(8,128)(2,1)}, b...) custom-call(bf16[512,4096]{1,0:T(8,128)(2,1)} %x.3, ...), custom_call_target="tpu_custom_call" | custom-call | tf_op jit(solution)/shard_map/pallas_call | solution.py:408
  265.7 3.0 collective-permute-start
  268.8 0.7 collective-permute-start.1
  269.5 0.0 copy-start
  269.5 0.0 copy-start.1
  269.5 22.1 %shard_map.47._ = f32[4096,4096]{1,0:T(8,128)} custom-call(bf16[512,4096]{1,0:T(8,128)(2,1)} %x.3, bf16[2048,4096]{1,0:T(8,128)(2,1)} %get-tuple-element.15.xz, bf16[2048,4096]{1,0:T(8,128)(2,1)} %get-tuple-element.16.xb, bf16[4096,2048]{1,0:T(8,128)(2,1)S(1)} %get-tuple-element.17.lhs, bf16[4096,3328]{1,0:T(8,128)(2,1)S(1)} %get-tuple-element.18.kept), custom_call_target="tpu_custom_call" | custom-call | flops 10000000000 | bytes 67108864 | tf_op jit(solution)/shard_map/pallas_call | solution.py:482
  291.5 0.0 collective-permute-done.got_h
  291.5 0.0 collective-permute-done.1.got_o
  291.6 0.0 copy-start.2
  291.6 0.8 copy-done.2
  292.4 0.0 copy-done
  292.4 0.0 copy-done.1
  292.4 9.6 %shard_map.48 = f32[4096,4096]{1,0:T(8,128)} custom-call(bf16[4096,2048]{1,0:T(8,128)(2,1)} %get-tuple-element.12.lhs_in, bf16[1024,256]{1,0:T(8,128)(2,1)S(1)} %copy-done, bf16[1024,256]{1,0:T(8,128)(2,1)S(1)} %copy-done.1, bf16[1024,256]{1,0:T(8,128)(2,1)S(1)} %collective-permute-done.got_h, ...), custom_call_target="tpu_custom_call", output_to_operand_aliasing={{}: (5, {})} | custom-call | tf_op jit(solution)/shard_map/pallas_call | solution.py:540
Async XLA Ops:
  265.7 25.8 %collective-permute-start = (bf16[1024,256]{1,0:T(8,128)(2,1)}, bf16[1024,256]{1,0:T(8,128)(2,1)S(1)}, u32[]{:S(2)}, u32[]{:S(2)}) collective-permute-start(bf16[1024,256]{1,0:T(8,128)(2,1)} %get-tuple-element.13.tail_h), channel_id=1, source_target_pairs={{2,3},{5,4},{6,7},{9,8},{10,11},{13,12},{18,19},{21,20},{22,23},{2... | collective-permute-start | bytes 1572872 | tf_op jit(solution)/shard_map/ppermute | solution.py:583
  268.8 22.8 %collective-permute-start.1 = (bf16[1024,256]{1,0:T(8,128)(2,1)}, bf16[1024,256]{1,0:T(8,128)(2,1)S(1)}, u32[]{:S(2)}, u32[]{:S(2)}) collective-permute-start(bf16[1024,256]{1,0:T(8,128)(2,1)} %get-tuple-element.14.tail_o), channel_id=1, source_target_pairs={{5,4},{6,7},{9,8},{10,11},{21,20},{22,23},{25,24},{26,27}} | collective-permute-start | bytes 1572872 | tf_op jit(solution)/shard_map/ppermute | solution.py:584
  269.5 22.9 %copy-start = (bf16[1024,256]{1,0:T(8,128)(2,1)S(1)}, bf16[1024,256]{1,0:T(8,128)(2,1)}, u32[]{:S(2)}) copy-start(bf16[1024,256]{1,0:T(8,128)(2,1)} %get-tuple-element.13.tail_h) | copy-start | bytes 1572868
  269.5 22.9 %copy-start.1 = (bf16[1024,256]{1,0:T(8,128)(2,1)S(1)}, bf16[1024,256]{1,0:T(8,128)(2,1)}, u32[]{:S(2)}) copy-start(bf16[1024,256]{1,0:T(8,128)(2,1)} %get-tuple-element.14.tail_o) | copy-start | bytes 1572868
  291.6 0.8 copy-start.2

commit v4 on v3

--- a/solution.py
+++ b/solution.py
@@ -12,7 +12,7 @@
 UNITS = 16
 TILES = 8
 EARLY = 13
-FIRST = CHUNKS + 11
+FIRST = CHUNKS + 7
 HELD = 3 * CHUNKS // 4
 TICKS = 3 * CHUNKS + 4
 PER_TICK = 64 // CHUNKS
@@ -21,7 +21,7 @@
 TAIL = CHUNKS // 16
 CUT = CHUNKS - TAIL
 TO_SIB, TO_OPP, UP, DOWN, FWD, DOWN_OPP, UP_OPP, UP_DIA, HOP_OWN, HOP_SIB, HOP_OPP, HOP_DIA, PASS, CROSS, SIDE, SIDE_CROSS = range(16)
-SLOTS = 6
+SLOTS = 7
 STRIPS = 4
 
 
@@ -493,7 +493,7 @@
             pltpu.SemaphoreType.DMA((SLOTS,)),
         ],
         cost_estimate=pl.CostEstimate(flops=10**10, bytes_accessed=cols * cols * 4, transcendentals=0),
-        compiler_params=pltpu.CompilerParams(vmem_limit_bytes=16 * MIB),
+        compiler_params=pltpu.CompilerParams(vmem_limit_bytes=17 * MIB),
     )(pair_block, xz, xb, lhs, kept)
 
 
@@ -551,7 +551,7 @@
             pltpu.SemaphoreType.DMA((2,)),
         ],
         input_output_aliases={5: 0},
-        compiler_params=pltpu.CompilerParams(vmem_limit_bytes=52 * MIB),
+        compiler_params=pltpu.CompilerParams(vmem_limit_bytes=49 * MIB),
     )(lhs, tail_h, tail_o, got_h, got_o, out)
 
 

time: 306 us -> 305 us (level)
  no operation moved by 1% of the time
where the time goes in v4:
time: 305 us; the launch traced here: 301 us
  Pallas kernels  295 us (97%)
  starting transfers between devices  5.12 us (2%)
    pallas_call x1, Pallas kernels, gather(): pl.pallas_call(gather_kernel, out_shape=(full, full, block, block, half,...  263 us
    pallas_call x1, Pallas kernels, finish(): pl.pallas_call(finish_kernel, out_shape=jax.ShapeDtypeStruct((cols, cols)...  22.1 us
    pallas_call x1, Pallas kernels, close(): pl.pallas_call(tail_kernel, out_shape=jax.ShapeDtypeStruct(out.shape, out...  9.57 us
  transfers between devices with their start and end apart: 2, of which 0 were waited for; matrix products, arithmetic and copies ran while one was open for 0% of the time, Pallas kernels for 7%

profile of v4, /device:TPU:16, one launch (start us, length us, event | category | flops | bytes accessed | tf_op | source)
XLA Modules:
  0.0 301.2 jit_solution(8147794016591071804)
XLA Ops:
  1.3 263.0 %shard_map.46 = (bf16[2048,4096]{1,0:T(8,128)(2,1)}, bf16[2048,4096]{1,0:T(8,128)(2,1)}, bf16[512,4096]{1,0:T(8,128)(2,1)}, bf16[512,4096]{1,0:T(8,128)(2,1)}, b...) custom-call(bf16[512,4096]{1,0:T(8,128)(2,1)} %x.3, ...), custom_call_target="tpu_custom_call" | custom-call | tf_op jit(solution)/shard_map/pallas_call | solution.py:408
  264.3 4.4 %collective-permute-start = (bf16[1024,256]{1,0:T(8,128)(2,1)}, bf16[1024,256]{1,0:T(8,128)(2,1)S(1)}, u32[]{:S(2)}, u32[]{:S(2)}) collective-permute-start(bf16[1024,256]{1,0:T(8,128)(2,1)} %get-tuple-element.13.tail_h), channel_id=1, source_target_pairs={{2,3},{5,4},{6,7},{9,8},{10,11},{13,12},{18,19},{21,20},{22,23},{2... | collective-permute-start | bytes 1572872 | tf_op jit(solution)/shard_map/ppermute | solution.py:583
  268.8 0.7 collective-permute-start.1
  269.5 0.0 copy-start
  269.5 0.0 copy-start.1
  269.5 22.1 %shard_map.47._ = f32[4096,4096]{1,0:T(8,128)} custom-call(bf16[512,4096]{1,0:T(8,128)(2,1)} %x.3, bf16[2048,4096]{1,0:T(8,128)(2,1)} %get-tuple-element.15.xz, bf16[2048,4096]{1,0:T(8,128)(2,1)} %get-tuple-element.16.xb, bf16[4096,2048]{1,0:T(8,128)(2,1)S(1)} %get-tuple-element.17.lhs, bf16[4096,3328]{1,0:T(8,128)(2,1)S(1)} %get-tuple-element.18.kept), custom_call_target="tpu_custom_call" | custom-call | flops 10000000000 | bytes 67108864 | tf_op jit(solution)/shard_map/pallas_call | solution.py:482
  291.5 0.0 collective-permute-done.got_h
  291.6 0.0 collective-permute-done.1.got_o
  291.6 0.0 copy-done
  291.6 0.0 copy-done.1
  291.6 9.6 %shard_map.48 = f32[4096,4096]{1,0:T(8,128)} custom-call(bf16[4096,2048]{1,0:T(8,128)(2,1)} %get-tuple-element.12.lhs_in, bf16[1024,256]{1,0:T(8,128)(2,1)S(1)} %copy-done, bf16[1024,256]{1,0:T(8,128)(2,1)S(1)} %copy-done.1, bf16[1024,256]{1,0:T(8,128)(2,1)S(1)} %collective-permute-done.got_h, ...), custom_call_target="tpu_custom_call", output_to_operand_aliasing={{}: (5, {})} | custom-call | tf_op jit(solution)/shard_map/pallas_call | solution.py:540
Async XLA Ops:
  264.3 27.2 %collective-permute-start = (bf16[1024,256]{1,0:T(8,128)(2,1)}, bf16[1024,256]{1,0:T(8,128)(2,1)S(1)}, u32[]{:S(2)}, u32[]{:S(2)}) collective-permute-start(bf16[1024,256]{1,0:T(8,128)(2,1)} %get-tuple-element.13.tail_h), channel_id=1, source_target_pairs={{2,3},{5,4},{6,7},{9,8},{10,11},{13,12},{18,19},{21,20},{22,23},{2... | collective-permute-start | bytes 1572872 | tf_op jit(solution)/shard_map/ppermute | solution.py:583
  268.8 22.8 %collective-permute-start.1 = (bf16[1024,256]{1,0:T(8,128)(2,1)}, bf16[1024,256]{1,0:T(8,128)(2,1)S(1)}, u32[]{:S(2)}, u32[]{:S(2)}) collective-permute-start(bf16[1024,256]{1,0:T(8,128)(2,1)} %get-tuple-element.14.tail_o), channel_id=1, source_target_pairs={{5,4},{6,7},{9,8},{10,11},{21,20},{22,23},{25,24},{26,27}} | collective-permute-start | bytes 1572872 | tf_op jit(solution)/shard_map/ppermute | solution.py:584
  269.5 22.1 %copy-start = (bf16[1024,256]{1,0:T(8,128)(2,1)S(1)}, bf16[1024,256]{1,0:T(8,128)(2,1)}, u32[]{:S(2)}) copy-start(bf16[1024,256]{1,0:T(8,128)(2,1)} %get-tuple-element.13.tail_h) | copy-start | bytes 1572868
  269.5 22.1 %copy-start.1 = (bf16[1024,256]{1,0:T(8,128)(2,1)S(1)}, bf16[1024,256]{1,0:T(8,128)(2,1)}, u32[]{:S(2)}) copy-start(bf16[1024,256]{1,0:T(8,128)(2,1)} %get-tuple-element.14.tail_o) | copy-start | bytes 1572868
